TPU v7x, 256 devices: a 2x2x32 block of a 4x8x32 slice. The times are simulated.
256 devices in a mesh: cohort: 4 (over x, y), tile: 64 (over z, core).
Axes of the slice: x: 2, y: 2, z: 32, core: 2. Of those that a mesh axis runs over, the one named last changes fastest.
The devices are a block of a 4x8x32 slice.
Arguments:
- dosage: bfloat16 [4096, 8192], P(('cohort', 'tile')), parts along dimension 0, may hold values from 0 to 2
- covars: float32 [4096, 16], P(('cohort', 'tile')), parts along dimension 0, may hold values from -12 to 12, as said below
- phenotypes: float32 [4096, 7168], P(('cohort', 'tile')), parts along dimension 0, may hold values from -100 to 100
Outputs:
- mean_chi: float32 [28672], P(('cohort', 'tile')), parts along dimension 0
- hit_rate: float32 [28672], P(('cohort', 'tile')), parts along dimension 0
There are 4 independent parts, one for each index of `cohort`. A program takes and returns all parts, laid end to end along the dimension named above; each array names one. Nothing has to cross between parts.
Inputs may be any that keep to these rules, and one draw needn't show every extreme that they name: `covars`: each covariate column has its own mean and spread.
All inputs are finite; a program needn't handle non-finite values.
Results may differ from a plain program's by a relative error of at most 0.003.
Values may be sent and summed in bfloat16 or wider, within the bound.
A program may use at most 64 MiB of HBM per device.

v0:
```python
import jax
import jax.numpy as jnp
from jax import lax
from jax.sharding import Mesh
from jax.sharding import PartitionSpec as P

TILE = ("tile_0", "tile_1")
COHORT_TILE = ("cohort", "tile_0", "tile_1")


def in_order(parts, dim):
    shape = list(parts.shape[1:])
    shape[dim] *= parts.shape[0]
    return jnp.moveaxis(parts, 0, dim).reshape(shape)


def gather_in_order(shard, axes, turns):
    parts = shard
    for k in turns:
        parts = lax.all_gather(parts, axes[k])
    done = turns[::-1]
    back = [done.index(k) for k in range(len(axes))]
    parts = parts.transpose(*back, *range(len(axes), parts.ndim))
    return parts.reshape(-1, *shard.shape)


def whole_of(shard, axes, turns, dim):
    return in_order(gather_in_order(shard, axes, turns), dim)


def local(dosage, covars, phenotypes):
    highest = lax.Precision.HIGHEST
    devices = lax.axis_size(TILE)
    local_rows = dosage.shape[0]
    variants = dosage.shape[1]
    samples = local_rows * devices
    genes_all = phenotypes.shape[1]
    gene_own = genes_all // devices
    scale_root = jnp.sqrt(jnp.float32(samples))
    covars_all = whole_of(covars, TILE, (0, 1), 0)
    dose_all = lax.all_gather(dosage, TILE, axis=0, tiled=True)
    pheno_own = lax.all_to_all(phenotypes, TILE, split_axis=1, concat_axis=0, tiled=True)
    gram = jnp.dot(covars_all.T, covars_all, precision=highest, preferred_element_type=jnp.float32)
    factor = jnp.linalg.cholesky(gram)
    cov_pheno = jnp.dot(
        covars_all.T, pheno_own, precision=highest, preferred_element_type=jnp.float32
    )
    beta_pheno = jax.scipy.linalg.cho_solve((factor, True), cov_pheno)
    pheno_resid = pheno_own - jnp.dot(
        covars_all, beta_pheno, precision=highest, preferred_element_type=jnp.float32
    )
    pheno_sumsq = jnp.sum(pheno_resid * pheno_resid, axis=0)
    pheno_bf = pheno_resid.astype(jnp.bfloat16)
    pheno_var = pheno_sumsq / samples + 0.1
    width = 1024
    blocks = variants // width

    def one_block(index, totals):
        start = index * width
        dose_block = lax.dynamic_slice_in_dim(dose_all, start, width, 1).astype(jnp.float32)
        cov_dose = jnp.dot(
            covars_all.T, dose_block, precision=highest, preferred_element_type=jnp.float32
        )
        beta_dose = jax.scipy.linalg.cho_solve((factor, True), cov_dose)
        dose_resid = dose_block - jnp.dot(
            covars_all, beta_dose, precision=highest, preferred_element_type=jnp.float32
        )
        dose_var = jnp.sum(dose_resid * dose_resid, axis=0) / samples + 0.1
        cross = lax.dot_general(
            pheno_bf,
            dose_resid.astype(jnp.bfloat16),
            (((0,), (0,)), ((), ())),
            preferred_element_type=jnp.float32,
        )
        zscore = cross / (scale_root * jnp.sqrt(pheno_var[:, None] * dose_var[None, :]))
        chi_square = zscore * zscore
        return (
            totals[0] + jnp.sum(chi_square, axis=1),
            totals[1] + jnp.sum(jax.nn.sigmoid(2.0 * (chi_square - 4.0)), axis=1),
        )

    zeros = jnp.zeros((gene_own,), jnp.float32)
    chi_total, hit_total = lax.fori_loop(0, blocks, one_block, (zeros, zeros))
    return (chi_total / variants, 20.0 / variants * hit_total)


def solution(mesh):
    finer = Mesh(mesh.devices.reshape(mesh.shape["cohort"], 32, 2), ("cohort", "tile_0", "tile_1"))
    return jax.shard_map(
        local,
        mesh=finer,
        in_specs=(P(COHORT_TILE, None), P(COHORT_TILE, None), P(COHORT_TILE, None)),
        out_specs=(P(COHORT_TILE), P(COHORT_TILE)),
        check_vma=False,
    )
```

profile of v0, /device:TPU:37, one launch (start us, length us, event | category | flops | bytes accessed | tf_op | source)
XLA Modules:
  0.0 319.9 jit_solution(15411580369733609212)
XLA Ops:
  8.0 1.3 all_to_all.14
  10.4 34.3 %all-to-all-start = ((f32[16,64,112]{2,0,1:T(8,128)}), f32[16,64,112]{2,0,1:T(8,128)S(1)}, u32[]{:S(2)}, u32[]{:S(2)}) async-start(f32[16,64,112]{2,0,1:T(8,128)} %copy.19), calls=%async_computation | async-start | bytes 1048576 | tf_op jit(solution)/shard_map/all_to_all | solution.py:42
  44.8 96.4 %all-gather = f32[512,16]{1,0:T(8,128)S(1)} all-gather(f32[16,16]{1,0:T(8,128)} %param.6), channel_id=2, replica_groups=mesh['cohort'=4,'tile_0'=32,'tile_1'=2] {'tile_0'}, dimensions={0}, use_global_device_ids=true | all-gather | bytes 33792 | tf_op jit(solution)/shard_map/all_gather | solution.py:20
  141.2 9.8 %all-gather.1 = f32[64,16,16]{2,1,0:T(8,128)S(1)} all-gather(f32[32,16,16]{2,1,0:T(8,128)S(1)} %bitcast.97), channel_id=3, replica_groups=mesh['cohort'=4,'tile_0'=32,'tile_1'=2] {'tile_1'}, dimensions={0}, use_global_device_ids=true | all-gather | bytes 98304 | tf_op jit(solution)/shard_map/all_gather | solution.py:20
  151.8 1.5 cholesky.18
  159.2 55.1 %all-gather.4.cloned.1.call-done = bf16[1024,8192]{1,0:T(8,128)(2,1)} async-done(((bf16[16,8192]{1,0:T(8,128)(2,1)}), bf16[1024,8192]{1,0:T(8,128)(2,1)}) %all-gather.4.cloned.1.call-update) | async-done | bytes 16777232 | tf_op jit(solution)/shard_map/all_gather | solution.py:41
  214.3 98.2 %while.18 = (s32[]{:T(128)}, f32[112]{0:T(128)S(1)}, f32[112]{0:T(128)S(1)}, bf16[1024,8192]{1,0:T(8,128)(2,1)}, f32[16,16]{1,0:T(8,128)S(1)}, /*index=5*/f32[10...) while((s32[]{:T(128)}, f32[112]{0:T(128)S(1)}, ...), condition=%wide.region_7.8_spmd.clone, body=%wide.region_3.7_spmd.clone.sunk | while | flops 652428992 | bytes 15458425 | solution.py:83
  214.3 2.5 fusion.67
  216.8 1.2 custom-call.29
  218.5 5.4 %multiply_reduce_fusion.3 = (f32[1024]{0:T(1024)S(1)}, f32[1024,1024]{0,1:T(8,128)S(1)}) fusion(bf16[1024,8192]{1,0:T(8,128)(2,1)} %get-tuple-element.371, s32[]{:T(128)S(6)} %select_n.19, f32[16,1024]{1,0:T(8,128)S(1)} %fusion.69, f32[1024,16]{0,1:T(8,128)S(1)} %get-tuple-element.373), kind=kOutput, calls=%fused_computation.1.clone.1 | convolution fusion | flops 205519872 | bytes 6426628 | tf_op jit(solution)/shard_map/while/body/eval_jaxpr/dot_general | solution.py:65
  223.9 2.6 fusion.70
  226.5 2.5 fusion.67
  230.8 5.4 %multiply_reduce_fusion.3 = (f32[1024]{0:T(1024)S(1)}, f32[1024,1024]{0,1:T(8,128)S(1)}) fusion(bf16[1024,8192]{1,0:T(8,128)(2,1)} %get-tuple-element.371, s32[]{:T(128)S(6)} %select_n.19, f32[16,1024]{1,0:T(8,128)S(1)} %fusion.69, f32[1024,16]{0,1:T(8,128)S(1)} %get-tuple-element.373), kind=kOutput, calls=%fused_computation.1.clone.1 | convolution fusion | flops 205519872 | bytes 6426628 | tf_op jit(solution)/shard_map/while/body/eval_jaxpr/dot_general | solution.py:65
  236.2 2.6 fusion.70
  238.8 2.5 fusion.67
  243.1 5.4 %multiply_reduce_fusion.3 = (f32[1024]{0:T(1024)S(1)}, f32[1024,1024]{0,1:T(8,128)S(1)}) fusion(bf16[1024,8192]{1,0:T(8,128)(2,1)} %get-tuple-element.371, s32[]{:T(128)S(6)} %select_n.19, f32[16,1024]{1,0:T(8,128)S(1)} %fusion.69, f32[1024,16]{0,1:T(8,128)S(1)} %get-tuple-element.373), kind=kOutput, calls=%fused_computation.1.clone.1 | convolution fusion | flops 205519872 | bytes 6426628 | tf_op jit(solution)/shard_map/while/body/eval_jaxpr/dot_general | solution.py:65
  248.5 2.6 fusion.70
  251.1 2.5 fusion.67
  255.3 5.4 %multiply_reduce_fusion.3 = (f32[1024]{0:T(1024)S(1)}, f32[1024,1024]{0,1:T(8,128)S(1)}) fusion(bf16[1024,8192]{1,0:T(8,128)(2,1)} %get-tuple-element.371, s32[]{:T(128)S(6)} %select_n.19, f32[16,1024]{1,0:T(8,128)S(1)} %fusion.69, f32[1024,16]{0,1:T(8,128)S(1)} %get-tuple-element.373), kind=kOutput, calls=%fused_computation.1.clone.1 | convolution fusion | flops 205519872 | bytes 6426628 | tf_op jit(solution)/shard_map/while/body/eval_jaxpr/dot_general | solution.py:65
  260.8 2.6 fusion.70
  263.4 2.5 fusion.67
  267.6 5.4 %multiply_reduce_fusion.3 = (f32[1024]{0:T(1024)S(1)}, f32[1024,1024]{0,1:T(8,128)S(1)}) fusion(bf16[1024,8192]{1,0:T(8,128)(2,1)} %get-tuple-element.371, s32[]{:T(128)S(6)} %select_n.19, f32[16,1024]{1,0:T(8,128)S(1)} %fusion.69, f32[1024,16]{0,1:T(8,128)S(1)} %get-tuple-element.373), kind=kOutput, calls=%fused_computation.1.clone.1 | convolution fusion | flops 205519872 | bytes 6426628 | tf_op jit(solution)/shard_map/while/body/eval_jaxpr/dot_general | solution.py:65
  273.1 2.6 fusion.70
  275.7 2.5 fusion.67
  279.9 5.4 %multiply_reduce_fusion.3 = (f32[1024]{0:T(1024)S(1)}, f32[1024,1024]{0,1:T(8,128)S(1)}) fusion(bf16[1024,8192]{1,0:T(8,128)(2,1)} %get-tuple-element.371, s32[]{:T(128)S(6)} %select_n.19, f32[16,1024]{1,0:T(8,128)S(1)} %fusion.69, f32[1024,16]{0,1:T(8,128)S(1)} %get-tuple-element.373), kind=kOutput, calls=%fused_computation.1.clone.1 | convolution fusion | flops 205519872 | bytes 6426628 | tf_op jit(solution)/shard_map/while/body/eval_jaxpr/dot_general | solution.py:65
  285.4 2.6 fusion.70
  288.0 2.5 fusion.67
  292.2 5.4 %multiply_reduce_fusion.3 = (f32[1024]{0:T(1024)S(1)}, f32[1024,1024]{0,1:T(8,128)S(1)}) fusion(bf16[1024,8192]{1,0:T(8,128)(2,1)} %get-tuple-element.371, s32[]{:T(128)S(6)} %select_n.19, f32[16,1024]{1,0:T(8,128)S(1)} %fusion.69, f32[1024,16]{0,1:T(8,128)S(1)} %get-tuple-element.373), kind=kOutput, calls=%fused_computation.1.clone.1 | convolution fusion | flops 205519872 | bytes 6426628 | tf_op jit(solution)/shard_map/while/body/eval_jaxpr/dot_general | solution.py:65
  297.6 2.6 fusion.70
  300.2 2.5 fusion.67
  304.5 5.4 %multiply_reduce_fusion.3 = (f32[1024]{0:T(1024)S(1)}, f32[1024,1024]{0,1:T(8,128)S(1)}) fusion(bf16[1024,8192]{1,0:T(8,128)(2,1)} %get-tuple-element.371, s32[]{:T(128)S(6)} %select_n.19, f32[16,1024]{1,0:T(8,128)S(1)} %fusion.69, f32[1024,16]{0,1:T(8,128)S(1)} %get-tuple-element.373), kind=kOutput, calls=%fused_computation.1.clone.1 | convolution fusion | flops 205519872 | bytes 6426628 | tf_op jit(solution)/shard_map/while/body/eval_jaxpr/dot_general | solution.py:65
  309.9 2.6 fusion.70
  (71 shorter events, 21.5 us)
Async XLA Ops:
  7.2 207.1 %all-gather.4.cloned.1.call-start = ((), (), s32[]{:S(2)}) async-start(), calls=%async_computation.1 | async-start | bytes 17039360 | tf_op jit(solution)/shard_map/all_gather | solution.py:41
  10.4 147.0 %all-to-all-start = ((f32[16,64,112]{2,0,1:T(8,128)}), f32[16,64,112]{2,0,1:T(8,128)S(1)}, u32[]{:S(2)}, u32[]{:S(2)}) async-start(f32[16,64,112]{2,0,1:T(8,128)} %copy.19), calls=%async_computation | async-start | bytes 1048576 | tf_op jit(solution)/shard_map/all_to_all | solution.py:42
Sparse Core Ops, SparseCore 0:
  9.9 204.3 all-gather.3
where the time goes:
time: 321 us; the launch traced here: 320 us
  blocking collectives  106 us (33%)
  matrix products  89.5 us (28%)
  waiting for transfers between devices  55.8 us (17%)
  starting transfers between devices  34.4 us (11%)
  other arithmetic  14.6 us (5%)
  between operations  14.1 us (4%)
  local copies, waits for them, and re-layouts  4.66 us (1%)
    all_gather x2, blocking collectives, gather_in_order(): parts = lax.all_gather(parts, axes[k])  106 us
    all_gather x1, waiting for transfers between devices, local(): dose_all = lax.all_gather(dosage, TILE, axis=0, tiled=True)  55.1 us
    dot_general x8, matrix products, one_block(): jnp.dot(covars_all, beta_dose, precision=highest, preferred_element_type=...  43.4 us
    all_to_all x1, starting transfers between devices, local(): lax.all_to_all(phenotypes, TILE, split_axis=1, concat_axis=0, tiled=True)  34.3 us
    dot_general x8, matrix products, one_block(): lax.dot_general(pheno_bf, dose_resid.astype(jnp.bfloat16), (((0,), (0,)),...  20.5 us
    dot_general x8, matrix products, one_block(): jnp.dot(covars_all.T, dose_block, precision=highest, preferred_element_ty...  20.1 us
    another operation x16, other arithmetic, one_block(): beta_dose = jax.scipy.linalg.cho_solve((factor, True), cov_dose)  9.88 us
  transfers between devices with their start and end apart: 2, of which 1 were waited for; matrix products, arithmetic and copies ran while one was open for 3% of the time, Pallas kernels for 0%

commit v1 on v0

--- a/solution.py
+++ b/solution.py
@@ -6,6 +6,13 @@
 
 TILE = ("tile_0", "tile_1")
 COHORT_TILE = ("cohort", "tile_0", "tile_1")
+
+
+def link_keys(local_x, lane_axis):
+    return jnp.concatenate(
+        lax.all_to_all(jnp.stack([local_x] * lax.axis_size(lane_axis), axis=0), lane_axis, 0, 0),
+        axis=0,
+    )
 
 
 def in_order(parts, dim):
@@ -38,7 +45,7 @@
     gene_own = genes_all // devices
     scale_root = jnp.sqrt(jnp.float32(samples))
     covars_all = whole_of(covars, TILE, (0, 1), 0)
-    dose_all = lax.all_gather(dosage, TILE, axis=0, tiled=True)
+    dose_all = link_keys(dosage, TILE)
     pheno_own = lax.all_to_all(phenotypes, TILE, split_axis=1, concat_axis=0, tiled=True)
     gram = jnp.dot(covars_all.T, covars_all, precision=highest, preferred_element_type=jnp.float32)
     factor = jnp.linalg.cholesky(gram)

time: 321 us -> 1720 us (5.36)
  blocking collectives: 106 us -> 1590 us
  waiting for transfers between devices: 55.8 us -> 0.01 us
  starting transfers between devices: 34.4 us -> 7.53 us
    all_gather x2, blocking collectives: 106 us -> 1500 us  [gather_in_order(): parts = lax.all_gather(parts, axes[k])]
    all_to_all x0 -> x1, blocking collectives: none -> 98.1 us  [local(): lax.all_to_all(phenotypes, TILE, split_axis=1, concat_axis=0, tiled=True)]
    all_gather x1 -> x0, waiting for transfers between devices: 55.1 us -> none  [local(): dose_all = lax.all_gather(dosage, TILE, axis=0, tiled=True)]
    all_to_all x1, starting transfers between devices: 34.3 us -> 7.53 us  [link_keys(): lax.all_to_all(jnp.stack([local_x] * lax.axis_size(lane_axis), axis=0), l...]
  transfers between devices with their start and end apart: 2 -> 1, of which waited for: 1 -> 0; matrix products, arithmetic and copies ran while one was open for 3% -> 0% of each run, Pallas kernels for 0% -> 0%
where the time goes in v1:
time: 1720 us
  blocking collectives  1590 us (92%)
  matrix products  89.6 us (5%)
    all_gather x2, blocking collectives, gather_in_order(): parts = lax.all_gather(parts, axes[k])  1500 us
    all_to_all x1, blocking collectives, local(): lax.all_to_all(phenotypes, TILE, split_axis=1, concat_axis=0, tiled=True)  98.1 us
    dot_general x8, matrix products, one_block(): jnp.dot(covars_all, beta_dose, precision=highest, preferred_element_type=...  43.4 us
  transfers between devices with their start and end apart: 1, of which 0 were waited for; matrix products, arithmetic and copies ran while one was open for 0% of the time, Pallas kernels for 0%

profile of v1, /device:TPU:37, one launch (start us, length us, event | category | flops | bytes accessed | tf_op | source)
XLA Modules:
  0.0 1717.4 jit_solution(7346706548844746509)
XLA Ops:
  0.6 1.3 all_to_all.18
  2.3 98.1 %all_to_all.24 = f32[16,64,112]{2,0,1:T(8,128)S(1)} all-to-all(f32[16,64,112]{2,0,1:T(8,128)S(1)} %copy.19), channel_id=1, replica_groups=mesh['cohort'=4,'tile_0'=32,'tile_1'=2] {'tile_0','tile_1'}, dimensions={1} | all-to-all | bytes 917504 | tf_op jit(solution)/shard_map/all_to_all | solution.py:49
  100.4 6.7 stack.2
  107.1 7.5 all-to-all-start
  114.6 1480.3 %all-gather = f32[512,16]{1,0:T(8,128)S(1)} all-gather(f32[16,16]{1,0:T(8,128)S(1)} %copy-done), channel_id=2, replica_groups=mesh['cohort'=4,'tile_0'=32,'tile_1'=2] {'tile_0'}, dimensions={0}, use_global_device_ids=true | all-gather | bytes 33792 | tf_op jit(solution)/shard_map/all_gather | solution.py:27
  1594.9 15.5 all-gather.1
  1611.2 1.5 cholesky.18
  1618.6 98.3 %while.18 = (s32[]{:T(128)}, f32[112]{0:T(128)S(1)}, f32[112]{0:T(128)S(1)}, bf16[1024,8192]{1,0:T(8,128)(2,1)}, f32[16,16]{1,0:T(8,128)S(1)}, /*index=5*/f32[10...) while((s32[]{:T(128)}, f32[112]{0:T(128)S(1)}, ...), condition=%wide.region_7.8_spmd.clone, body=%wide.region_3.7_spmd.clone.sunk | while | flops 652428992 | bytes 15458433 | solution.py:90
  1618.6 2.5 fusion.67
  1622.9 5.4 multiply_reduce_fusion.3
  1628.3 2.6 fusion.70
  1630.9 2.5 fusion.67
  1635.1 5.4 multiply_reduce_fusion.3
  1640.6 2.6 fusion.70
  1643.2 2.5 fusion.67
  1647.4 5.4 multiply_reduce_fusion.3
  1652.9 2.6 fusion.70
  1655.5 2.5 fusion.67
  1659.7 5.4 multiply_reduce_fusion.3
  1665.2 2.6 fusion.70
  1667.8 2.5 fusion.67
  1672.0 5.4 multiply_reduce_fusion.3
  1677.4 2.6 fusion.70
  1680.0 2.5 fusion.67
  1684.3 5.4 multiply_reduce_fusion.3
  1689.7 2.6 fusion.70
  1692.3 2.5 fusion.67
  1696.6 5.4 multiply_reduce_fusion.3
  1702.0 2.6 fusion.70
  1704.6 2.5 fusion.67
  1708.9 5.4 multiply_reduce_fusion.3
  1714.3 2.6 fusion.70
  (72 shorter events, 21.2 us)
Async XLA Ops:
  107.1 7.6 copy-start
  107.1 1511.5 %all-to-all-start = ((bf16[64,16,8192]{2,1,0:T(8,128)(2,1)}), bf16[64,16,8192]{2,1,0:T(8,128)(2,1)}, u32[]{:S(2)}, u32[]{:S(2)}) async-start(bf16[64,16,8192]{2,1,0:T(8,128)(2,1)} %stack.2), calls=%async_computation | async-start | bytes 33554432 | tf_op jit(solution)/shard_map/all_to_all | solution.py:13
